TPU v7x, 32 devices: a whole 2x2x4 slice. The times are simulated.
32 devices in a mesh: seq: 8 (over z, y), tensor: 4 (over x, core).
Axes of the slice: x: 2, y: 2, z: 4, core: 2. Of those that a mesh axis runs over, the one named last changes fastest.
Arguments:
- layer_input: bfloat16 [2048, 4096], P('seq', 'tensor'), may hold values from -6 to 6
- norm_gain: float32 [4096], replicated, may hold values from 0.1 to 1.9
- in_weights: bfloat16 [2, 4096, 2048], P(None, None, 'tensor'), may hold values from -0.09375 to 0.09375
- conv_weight: float32 [4, 2048], P(None, 'tensor'), may hold values from -4 to 4
- conv_bias: float32 [2048], P('tensor'), may hold values from -3 to 3
- gate_weights: bfloat16 [2, 8, 256, 256], P(None, 'tensor'), may hold values from -0.375 to 0.375
- gate_bias: float32 [2, 2048], P(None, 'tensor'), may hold values from -4 to 4
- decay_rate: float32 [2048], P('tensor'), may hold values from 1e-06 to 0.03, as said below
- out_weight: bfloat16 [2048, 4096], P('tensor'), may hold values from -0.1875 to 0.1875
- mlp_gain: float32 [4096], replicated, may hold values from 0.1 to 1.9
- mlp_in: bfloat16 [2, 4096, 6144], P(None, 'seq', 'tensor'), may hold values from -0.09375 to 0.09375
- mlp_out: bfloat16 [6144, 4096], P('tensor', 'seq'), may hold values from -0.109375 to 0.109375
Outputs:
- block_output: bfloat16 [2048, 4096], P('seq', 'tensor')
Inputs may be any that keep to these rules, and one draw needn't show every extreme that they name: `decay_rate`: every rate is positive.
All inputs are finite; a program needn't handle non-finite values.
Results may differ from a plain program's by a relative error of at most 0.015.
Values may be sent and summed in bfloat16 or wider, within the bound.
A program may use at most 128 MiB of HBM per device.

v0:
```python
import jax
import jax.numpy as jnp
from jax import lax
from jax.sharding import PartitionSpec as P


def shifted(value, axis, steps):
    count = lax.axis_size(axis)
    first, last = (max(0, -steps), min(count, count - steps))
    return lax.ppermute(value, axis, [(source, source + steps) for source in range(first, last)])


def prefix(value, axis, combine, identity):
    size, here = (lax.axis_size(axis), lax.axis_index(axis))
    everything = jax.tree.map(lambda part: lax.all_gather(part, axis), value)
    start = jax.tree.map(
        lambda part, zero: jnp.broadcast_to(jnp.asarray(zero, part.dtype), part.shape),
        value,
        identity,
    )

    def hop(k, before):
        reached = k < here
        new = combine(before, jax.tree.map(lambda part: part[k], everything))
        return jax.tree.map(lambda a, b: jnp.where(reached, a, b), new, before)

    return lax.fori_loop(0, size, hop, start)


def rms_scale(rows, gain):
    values = rows.astype(jnp.float32)
    mean_square = jnp.mean(values * values, axis=-1, keepdims=True)
    return (values * lax.rsqrt(mean_square + 1e-06) * gain).astype(jnp.bfloat16)


def chain_step(earlier, later):
    return (earlier[0] * later[0], later[0] * earlier[1] + later[1])


def shards(
    layer_input,
    norm_gain,
    in_weights,
    conv_weight,
    conv_bias,
    gate_weights,
    gate_bias,
    decay_rate,
    out_weight,
    mlp_gain,
    mlp_in,
    mlp_out,
):
    whole_rows = lax.all_gather(layer_input, "tensor", axis=1, tiled=True)
    normed = rms_scale(whole_rows, norm_gain)
    branch_x = jnp.dot(normed, in_weights[0], preferred_element_type=jnp.float32).astype(
        jnp.bfloat16
    )
    branch_y = jax.nn.gelu(
        jnp.dot(normed, in_weights[1], preferred_element_type=jnp.float32), approximate=True
    )
    num_tokens = branch_x.shape[0]
    rim_rows = conv_weight.shape[0] - 1
    earlier_rows = shifted(branch_x[num_tokens - rim_rows :], "seq", 1)
    padded = jnp.concatenate([earlier_rows, branch_x], axis=0).astype(jnp.float32)
    convolved = jnp.zeros(branch_x.shape, jnp.float32) + conv_bias
    for tap_index in range(conv_weight.shape[0]):
        start_row = rim_rows - tap_index
        convolved = convolved + conv_weight[tap_index] * padded[start_row : start_row + num_tokens]
    conv_out = convolved.astype(jnp.bfloat16)
    local_blocks = gate_weights.shape[1]
    block_width = gate_weights.shape[2]
    blocks_in = conv_out.reshape(num_tokens, local_blocks, block_width)
    gate_pre = jnp.einsum(
        "tnc,knce->ktne", blocks_in, gate_weights, preferred_element_type=jnp.float32
    )
    gate_pre = gate_pre.reshape(2, num_tokens, local_blocks * block_width) + gate_bias[:, None, :]
    log_decay = -8.0 * jax.nn.sigmoid(gate_pre[0]) * decay_rate
    decay = jnp.exp(log_decay)
    driven = (
        conv_out.astype(jnp.float32)
        * jax.nn.sigmoid(gate_pre[1])
        * jnp.sqrt(-jnp.expm1(2.0 * log_decay))
    )
    cum_decay, cum_state = lax.associative_scan(chain_step, (decay, driven), axis=0)
    identity = (jnp.ones_like(cum_decay[-1]), jnp.zeros_like(cum_state[-1]))
    entering = prefix((cum_decay[-1], cum_state[-1]), "seq", chain_step, identity)
    carried = entering[1]
    state = cum_decay * carried + cum_state
    mixed = (state * branch_y).astype(jnp.bfloat16)
    partial_sums = jnp.dot(mixed, out_weight, preferred_element_type=jnp.float32)
    full_sums = lax.psum(partial_sums.astype(jnp.bfloat16), "tensor").astype(jnp.float32)
    mid_full = (whole_rows.astype(jnp.float32) + full_sums).astype(jnp.bfloat16)
    own_width = layer_input.shape[1]
    residual = lax.dynamic_slice_in_dim(
        mid_full, lax.axis_index("tensor") * own_width, own_width, 1
    )
    mlp_normed = rms_scale(mid_full, mlp_gain)
    gate_up = jnp.einsum(
        "tr,krf->ktf",
        mlp_normed,
        lax.all_gather(mlp_in, "seq", axis=1, tiled=True),
        preferred_element_type=jnp.float32,
    )
    hidden = (jax.nn.gelu(gate_up[0], approximate=True) * gate_up[1]).astype(jnp.bfloat16)
    down_terms = jnp.dot(
        hidden,
        lax.all_gather(mlp_out, "seq", axis=1, tiled=True),
        preferred_element_type=jnp.float32,
    )
    down_share = lax.psum_scatter(
        down_terms.astype(jnp.bfloat16), "tensor", scatter_dimension=1, tiled=True
    ).astype(jnp.float32)
    return (residual.astype(jnp.float32) + down_share).astype(jnp.bfloat16)


def solution(mesh):
    return jax.shard_map(
        shards,
        mesh=mesh,
        in_specs=(
            P("seq", "tensor"),
            P(),
            P(None, None, "tensor"),
            P(None, "tensor"),
            P("tensor"),
            P(None, "tensor", None, None),
            P(None, "tensor"),
            P("tensor"),
            P("tensor", None),
            P(),
            P(None, "seq", "tensor"),
            P("tensor", "seq"),
        ),
        out_specs=P("seq", "tensor"),
        check_vma=False,
    )
```

profile of v0, /device:TPU:0, one launch (start us, length us, event | category | flops | bytes accessed | tf_op | source)
XLA Modules:
  0.0 835.9 jit_solution(12491428809460878877)
XLA Ops:
  7.4 0.0 copy-start
  7.4 0.7 all-gather.6.cloned.1.call-update
  8.1 0.0 all-reduce.34.cloned.1.call-start
  8.1 0.9 fusion.115
  9.0 26.0 %all-gather.6.cloned.1.call-done = bf16[256,4096]{1,0:T(8,128)(2,1)} async-done(((bf16[256,1024]{1,0:T(8,128)(2,1)}), bf16[256,4096]{1,0:T(8,128)(2,1)}) %all-gather.6.cloned.1.call-update) | async-done | bytes 2097168 | tf_op jit(solution)/shard_map/all_gather | solution.py:54
  35.0 2.1 fusion.3
  37.1 0.0 copy-start.6
  37.1 0.0 copy-start.4
  37.2 4.1 fusion.26
  41.3 3.4 collective-permute-start
  44.7 1.3 collective-permute-done
  46.0 0.1 maximum_convert_fusion
  46.1 0.3 fusion.73
  46.4 0.1 reshape.40
  46.4 0.0 copy-start.5
  46.5 0.0 copy-done
  46.5 0.3 convolution_bitcast_fusion.1
  46.8 0.6 copy.18
  47.4 0.8 reshape.41
  48.3 0.1 broadcast_add_fusion
  48.4 0.8 fusion.91
  49.2 0.3 slice.293
  49.5 0.3 slice.294
  49.8 0.3 slice.332
  50.2 0.3 slice.333
  50.5 0.1 fusion.108
  50.6 0.1 slice.296
  50.7 0.1 slice.297
  50.8 0.1 slice.335
  50.9 0.1 slice.336
  52.0 0.2 slice.326
  52.2 0.2 slice.365
  52.4 1.4 slice.328
  53.8 1.4 slice.367
  56.0 0.1 add_multiply_fusion.3
  56.2 1.7 pad.129
  58.1 0.0 copy-start.7
  58.1 2.0 add_multiply_fusion.1
  60.2 1.7 pad.128
  61.8 0.7 add_bitcast_fusion
  62.5 27.9 %all-gather.1 = f32[8,1,512]{2,1,0:T(1,128)S(1)} all-gather(f32[1,1,512]{2,1,0:T(1,128)S(1)} %add_bitcast_fusion), channel_id=1, replica_groups=mesh['seq'=8,'tensor'=4] {'seq'}, dimensions={0}, use_global_device_ids=true | all-gather | bytes 18432 | tf_op jit(solution)/shard_map/all_gather | solution.py:15
  90.4 1.6 pad.113
  92.1 1.0 pad_maximum_fusion
  93.1 1.7 pad.112
  94.7 0.7 add_bitcast_fusion.1
  95.5 26.1 %all-gather = f32[8,1,512]{2,1,0:T(1,128)S(1)} all-gather(f32[1,1,512]{2,1,0:T(1,128)S(1)} %add_bitcast_fusion.1), channel_id=1, replica_groups=mesh['seq'=8,'tensor'=4] {'seq'}, dimensions={0}, use_global_device_ids=true | all-gather | bytes 18432 | tf_op jit(solution)/shard_map/all_gather | solution.py:15
  121.6 0.4 while.14
  122.0 7.9 convolution_convert_fusion.1
  130.0 0.0 all-reduce.34.cloned.1.call-update
  130.0 0.0 all-gather.8.cloned.1.call-start
  130.0 0.5 all-gather.8.cloned.1.call-update
  130.6 0.0 all-gather.10.cloned.1.call-start
  130.6 0.5 all-gather.10.cloned.1.call-update
  131.2 0.0 copy-start.8
  131.2 0.2 reduce-scatter.2.cloned.1.call-start
  131.4 46.4 %all-reduce.34.cloned.1.call-done = bf16[256,4096]{1,0:T(8,128)(2,1)} async-done(((bf16[256,4096]{1,0:T(8,128)(2,1)}), bf16[256,4096]{1,0:T(8,128)(2,1)}) %all-reduce.34.cloned.1.call-update) | async-done | bytes 2097168 | tf_op jit(solution)/shard_map/psum | solution.py:92
  177.8 3.9 fusion
  181.7 427.0 %all-gather.8.cloned.1.call-done = bf16[2,4096,1536]{2,1,0:T(8,128)(2,1)} async-done(((bf16[2,512,1536]{2,1,0:T(8,128)(2,1)}), bf16[2,4096,1536]{2,1,0:T(8,128)(2,1)}) %all-gather.8.cloned.1.call-update) | async-done | bytes 25165840 | tf_op jit(solution)/shard_map/all_gather | solution.py:102
  608.7 13.4 %convolution_bitcast_fusion = f32[2,256,1536]{2,1,0:T(8,128)} fusion(bf16[2,4096,1536]{2,1,0:T(8,128)(2,1)} %all-gather.8.cloned.1.call-done, bf16[256,4096]{1,0:T(8,128)(2,1)} %get-tuple-element.129, f32[4096]{0:T(1024)S(1)} %copy-done.8, f32[256]{0:T(256)S(1)} %add_rsqrt_fusion), kind=kOutput, calls=%fused_computation.23 | convolution fusion | flops 6446645248 | bytes 30426112 | tf_op jit(solution)/shard_map/tr,krf->ktf/dot_general | solution.py:99
  622.1 164.4 %all-gather.10.cloned.1.call-done = bf16[1536,4096]{1,0:T(8,128)(2,1)} async-done(((bf16[1536,512]{1,0:T(8,128)(2,1)}), bf16[1536,4096]{1,0:T(8,128)(2,1)}) %all-gather.10.cloned.1.call-update) | async-done | bytes 12582928 | tf_op jit(solution)/shard_map/all_gather | solution.py:108
  786.5 10.6 %convolution_convert_fusion = bf16[256,4096]{1,0:T(8,128)(2,1)} fusion(bf16[1536,4096]{1,0:T(8,128)(2,1)} %all-gather.10.cloned.1.call-done, f32[2,256,1536]{2,1,0:T(8,128)} %convolution_bitcast_fusion), kind=kOutput, calls=%fused_computation.8 | convolution fusion | flops 3226206208 | bytes 17825792 | tf_op jit(solution)/shard_map/dot_general | solution.py:106
  797.1 0.0 reduce-scatter.2.cloned.1.call-update
  797.1 29.5 %reduce-scatter.2.cloned.1.call-done = bf16[256,1024]{1,0:T(8,128)(2,1)} async-done(((bf16[256,4096]{1,0:T(8,128)(2,1)}), bf16[256,1024]{1,0:T(8,128)(2,1)}) %reduce-scatter.2.cloned.1.call-update) | async-done | bytes 524304 | tf_op jit(solution)/shard_map/reduce_scatter | solution.py:111
  826.6 2.2 add_convert_fusion
  (136 shorter events, 1.9 us)
Async XLA Ops:
  7.4 39.1 %copy-start = (bf16[2,2,256,256]{3,2,1,0:T(8,128)(2,1)S(1)}, bf16[2,2,256,256]{3,2,1,0:T(8,128)(2,1)}, u32[]{:S(2)}) copy-start(bf16[2,2,256,256]{3,2,1,0:T(8,128)(2,1)} %param.19) | copy-start | bytes 1572868
  7.4 27.7 %all-gather.6.cloned.1.call-start = ((), (), s32[]{:S(2)}) async-start(), calls=%async_computation.1 | async-start | bytes 2621440 | tf_op jit(solution)/shard_map/all_gather | solution.py:54
  8.1 169.7 %all-reduce.34.cloned.1.call-start = ((), (), s32[]{:S(2)}) async-start(), calls=%async_computation.2 | async-start | bytes 4194304 | tf_op jit(solution)/shard_map/psum | solution.py:92
  37.1 7.6 copy-start.6
  37.1 9.0 %copy-start.4 = (f32[512]{0:T(512)S(1)}, f32[512]{0:T(512)}, u32[]{:S(2)}) copy-start(f32[512]{0:T(512)} %param.18) | copy-start | bytes 6148
  41.3 4.7 collective-permute-start
  46.4 1.8 copy-start.5
  58.1 63.9 %copy-start.2 = (bf16[256,4096]{1,0:T(8,128)(2,1)S(1)}, bf16[256,4096]{1,0:T(8,128)(2,1)}, u32[]{:S(2)}) copy-start(bf16[256,4096]{1,0:T(8,128)(2,1)} %all-gather.6.cloned.1.call-done) | copy-start | bytes 6291460
  58.1 63.9 %copy-start.7 = (f32[4096]{0:T(1024)S(1)}, f32[4096]{0:T(1024)}, u32[]{:S(2)}) copy-start(f32[4096]{0:T(1024)} %param.15) | copy-start | bytes 49156
  60.1 61.9 %copy-start.3 = (f32[256,512]{1,0:T(8,128)S(1)}, f32[256,512]{1,0:T(8,128)}, u32[]{:S(2)}) copy-start(f32[256,512]{1,0:T(8,128)} %pad.129) | copy-start | bytes 1572868
  130.0 478.7 %all-gather.8.cloned.1.call-start = ((), (), s32[]{:S(2)}) async-start(), calls=%async_computation.3 | async-start | bytes 28311552 | tf_op jit(solution)/shard_map/all_gather | solution.py:102
  130.6 656.0 %all-gather.10.cloned.1.call-start = ((), (), s32[]{:S(2)}) async-start(), calls=%async_computation.4 | async-start | bytes 14155776 | tf_op jit(solution)/shard_map/all_gather | solution.py:108
  131.2 477.6 %copy-start.8 = (f32[4096]{0:T(1024)S(1)}, f32[4096]{0:T(1024)}, u32[]{:S(2)}) copy-start(f32[4096]{0:T(1024)} %param.23) | copy-start | bytes 49156
  131.2 695.4 %reduce-scatter.2.cloned.1.call-start = ((), (), s32[]{:S(2)}) async-start(), calls=%async_computation.5 | async-start | bytes 2621440 | tf_op jit(solution)/shard_map/reduce_scatter | solution.py:111
  786.5 42.3 %copy-start.1 = (bf16[2,2,256,256]{3,2,1,0:T(8,128)(2,1)S(1)}, bf16[2,2,256,256]{3,2,1,0:T(8,128)(2,1)}, u32[]{:S(2)}) copy-start(bf16[2,2,256,256]{3,2,1,0:T(8,128)(2,1)} %param.19) | copy-start | bytes 1572868
Sparse Core Ops, SparseCore 0:
  9.7 25.2 all-gather.5
  130.1 47.6 all-reduce.33
  797.2 29.3 reduce-scatter.1
Sparse Core Ops, SparseCore 1:
  132.0 476.6 all-gather.7
  610.6 175.9 all-gather.9
where the time goes:
time: 836 us
  waiting for transfers between devices  696 us (83%)
  blocking collectives  54 us (6%)
  matrix products  36.4 us (4%)
  between operations  15.4 us (2%)
  local copies, waits for them, and re-layouts  15.1 us (2%)
  other arithmetic  14.7 us (2%)
    all_gather x1, waiting for transfers between devices, shards(): lax.all_gather(mlp_in, 'seq', axis=1, tiled=True)  427 us
    all_gather x1, waiting for transfers between devices, shards(): lax.all_gather(mlp_out, 'seq', axis=1, tiled=True)  164 us
    all_gather x2, blocking collectives, prefix(): everything = jax.tree.map(lambda part: lax.all_gather(part, axis), value)  54 us
    psum x1, waiting for transfers between devices, shards(): lax.psum(partial_sums.astype(jnp.bfloat16), 'tensor').astype(jnp.float32)  46.4 us
    reduce_scatter x1, waiting for transfers between devices, shards(): lax.psum_scatter(down_terms.astype(jnp.bfloat16), 'tensor', scatter_dimen...  29.5 us
    all_gather x1, waiting for transfers between devices, shards(): whole_rows = lax.all_gather(layer_input, 'tensor', axis=1, tiled=True)  26 us
  transfers between devices with their start and end apart: 6, of which 6 were waited for; matrix products, arithmetic and copies ran while one was open for 2% of the time, Pallas kernels for 0%

commit v1 on v0

--- a/solution.py
+++ b/solution.py
@@ -2,6 +2,22 @@
 import jax.numpy as jnp
 from jax import lax
 from jax.sharding import PartitionSpec as P
+
+
+def ring_product(x, axis, dim, contribution):
+    devices, mine, extent = (lax.axis_size(axis), lax.axis_index(axis), x.shape[dim])
+    right = [(i, (i + 1) % devices) for i in range(devices)]
+    left = [(i, (i - 1) % devices) for i in range(devices)]
+    halfway = devices // 2
+    from_left = from_right = x
+    total = contribution(x, mine * extent)
+    for step in range(1, halfway + 1):
+        from_left = lax.ppermute(from_left, axis, right)
+        if step < devices - halfway:
+            from_right = lax.ppermute(from_right, axis, left)
+            total = total + contribution(from_right, (mine + step) % devices * extent)
+        total = total + contribution(from_left, (mine - step) % devices * extent)
+    return total
 
 
 def shifted(value, axis, steps):
@@ -96,11 +112,16 @@
         mid_full, lax.axis_index("tensor") * own_width, own_width, 1
     )
     mlp_normed = rms_scale(mid_full, mlp_gain)
-    gate_up = jnp.einsum(
-        "tr,krf->ktf",
-        mlp_normed,
-        lax.all_gather(mlp_in, "seq", axis=1, tiled=True),
-        preferred_element_type=jnp.float32,
+    gate_up = ring_product(
+        mlp_in,
+        "seq",
+        1,
+        lambda part_2, offset: jnp.einsum(
+            "tr,krf->ktf",
+            lax.dynamic_slice_in_dim(mlp_normed, offset, part_2.shape[1], axis=1),
+            part_2,
+            preferred_element_type=jnp.float32,
+        ),
     )
     hidden = (jax.nn.gelu(gate_up[0], approximate=True) * gate_up[1]).astype(jnp.bfloat16)
     down_terms = jnp.dot(

time: 836 us -> 735 us (0.88)
  waiting for transfers between devices: 696 us -> 573 us
  starting transfers between devices: 3.72 us -> 19.9 us
    ppermute x0 -> x7, waiting for transfers between devices: none -> 517 us  [the longest x4 461 us: ring_product(): from_left = lax.ppermute(from_left, axis, right)]
    all_gather x1 -> x0, waiting for transfers between devices: 427 us -> none  [shards(): lax.all_gather(mlp_in, 'seq', axis=1, tiled=True)]
    all_gather x1, waiting for transfers between devices: 164 us -> 0.01 us  [shards(): lax.all_gather(mlp_out, 'seq', axis=1, tiled=True)]
    psum x1, waiting for transfers between devices: 46.4 us -> 0.01 us  [shards(): lax.psum(partial_sums.astype(jnp.bfloat16), 'tensor').astype(jnp.float32)]
    ppermute x0 -> x7, starting transfers between devices: none -> 16.4 us  [the longest x3 8.92 us: ring_product(): from_right = lax.ppermute(from_right, axis, left)]
    dot_general x1 -> x8, matrix products: 13.4 us -> 17.5 us  [shards(): jnp.einsum('tr,krf->ktf', lax.dynamic_slice_in_dim(mlp_normed, offset, pa...]
  transfers between devices with their start and end apart: 6 -> 12, of which waited for: 6 -> 8; matrix products, arithmetic and copies ran while one was open for 2% -> 3% of each run, Pallas kernels for 0% -> 0%
where the time goes in v1:
time: 735 us
  waiting for transfers between devices  573 us (78%)
  blocking collectives  54 us (7%)
  matrix products  40.5 us (6%)
  starting transfers between devices  19.9 us (3%)
  local copies, waits for them, and re-layouts  16.9 us (2%)
  between operations  15.5 us (2%)
  other arithmetic  14.6 us (2%)
    ppermute x4, waiting for transfers between devices, ring_product(): from_left = lax.ppermute(from_left, axis, right)  461 us
    ppermute x3, waiting for transfers between devices, ring_product(): from_right = lax.ppermute(from_right, axis, left)  55.8 us
    all_gather x2, blocking collectives, prefix(): everything = jax.tree.map(lambda part: lax.all_gather(part, axis), value)  54 us
    reduce_scatter x1, waiting for transfers between devices, shards(): lax.psum_scatter(down_terms.astype(jnp.bfloat16), 'tensor', scatter_dimen...  27.6 us
    all_gather x1, waiting for transfers between devices, shards(): whole_rows = lax.all_gather(layer_input, 'tensor', axis=1, tiled=True)  26 us
    dot_general x8, matrix products, shards(): jnp.einsum('tr,krf->ktf', lax.dynamic_slice_in_dim(mlp_normed, offset, pa...  17.5 us
  transfers between devices with their start and end apart: 12, of which 8 were waited for; matrix products, arithmetic and copies ran while one was open for 3% of the time, Pallas kernels for 0%

profile of v1, /device:TPU:0, one launch (start us, length us, event | category | flops | bytes accessed | tf_op | source)
XLA Modules:
  0.0 734.6 jit_solution(9497658108886503266)
XLA Ops:
  7.4 0.7 all-gather.5.cloned.1.call-update
  8.1 0.9 fusion.141
  9.0 26.0 %all-gather.5.cloned.1.call-done = bf16[256,4096]{1,0:T(8,128)(2,1)} async-done(((bf16[256,1024]{1,0:T(8,128)(2,1)}), bf16[256,4096]{1,0:T(8,128)(2,1)}) %all-gather.5.cloned.1.call-update) | async-done | bytes 2097168 | tf_op jit(solution)/shard_map/all_gather | solution.py:70
  35.0 2.1 fusion.3
  37.2 4.1 fusion.25
  41.3 3.4 collective-permute-start
  44.7 1.3 collective-permute-done
  46.1 0.3 fusion.72
  46.5 0.3 convolution_bitcast_fusion
  46.8 0.6 copy.18
  47.4 0.8 reshape.41
  48.3 0.1 broadcast_add_fusion
  48.4 0.8 fusion.109
  49.2 0.3 slice.293
  49.5 0.3 slice.294
  49.8 0.3 slice.332
  50.2 0.3 slice.333
  50.5 0.1 fusion.134
  50.6 0.1 slice.296
  50.7 0.1 slice.297
  50.8 0.1 slice.335
  50.9 0.1 slice.336
  52.0 0.2 slice.326
  52.2 0.2 slice.365
  52.4 1.4 slice.328
  53.8 1.4 slice.367
  56.3 1.6 pad.129
  58.1 2.0 add_multiply_fusion.1
  60.1 1.7 pad.128
  61.8 0.7 add_bitcast_fusion
  62.5 27.9 %all-gather.1 = f32[8,1,512]{2,1,0:T(1,128)S(1)} all-gather(f32[1,1,512]{2,1,0:T(1,128)S(1)} %add_bitcast_fusion), channel_id=1, replica_groups=mesh['seq'=8,'tensor'=4] {'seq'}, dimensions={0}, use_global_device_ids=true | all-gather | bytes 18432 | tf_op jit(solution)/shard_map/all_gather | solution.py:31
  90.4 1.7 pad.113
  92.2 1.0 pad_maximum_fusion
  93.1 1.7 pad.112
  94.8 0.7 add_bitcast_fusion.1
  95.6 26.1 %all-gather = f32[8,1,512]{2,1,0:T(1,128)S(1)} all-gather(f32[1,1,512]{2,1,0:T(1,128)S(1)} %add_bitcast_fusion.1), channel_id=1, replica_groups=mesh['seq'=8,'tensor'=4] {'seq'}, dimensions={0}, use_global_device_ids=true | all-gather | bytes 18432 | tf_op jit(solution)/shard_map/all_gather | solution.py:31
  121.7 0.4 while.14
  122.1 7.9 %convolution_convert_fusion.1 = bf16[256,4096]{1,0:T(8,128)(2,1)} fusion(bf16[512,4096]{1,0:T(8,128)(2,1)} %param.22, bf16[2,4096,512]{2,1,0:T(8,128)(2,1)} %param.16, bf16[256,4096]{1,0:T(8,128)(2,1)S(1)} %copy-done.2, f32[4096]{0:T(1024)S(1)} %copy-done.11, f32[256]{0:T(256)S(1)} %add_rsqrt_fusion.1, f32[256,512]{1,0:T(8,128)} %pad.128, ...), kind=kOutput, calls=%fused_computation.9 | convolution fusion | flops 2154561536 | bytes 14699520 | tf_op jit(solution)/shard_map/dot_general | solution.py:107
  130.1 0.5 all-gather.7.cloned.1.call-update
  130.8 4.7 collective-permute-start.1
  135.5 143.4 %collective-permute-done.2 = bf16[2,512,1536]{2,1,0:T(8,128)(2,1)S(1)} collective-permute-done((bf16[2,512,1536]{2,1,0:T(8,128)(2,1)}, bf16[2,512,1536]{2,1,0:T(8,128)(2,1)S(1)}, u32[]{:S(2)}, u32[]{:S(2)}) %collective-permute-start.2) | collective-permute-done | bytes 3145760 | tf_op jit(solution)/shard_map/ppermute | solution.py:15
  278.9 1.7 copy-done.3
  280.6 2.4 collective-permute-start.4
  283.0 0.3 collective-permute-done.1
  283.3 2.0 collective-permute-start.3
  285.3 189.8 %collective-permute-done.4 = bf16[2,512,1536]{2,1,0:T(8,128)(2,1)} collective-permute-done((bf16[2,512,1536]{2,1,0:T(8,128)(2,1)S(1)}, bf16[2,512,1536]{2,1,0:T(8,128)(2,1)}, u32[]{:S(2)}, u32[]{:S(2)}) %collective-permute-start.4) | collective-permute-done | bytes 3145760 | tf_op jit(solution)/shard_map/ppermute | solution.py:15
  475.1 2.6 collective-permute-start.6
  477.7 3.2 fusion
  481.0 2.2 collective-permute-start.5
  483.2 0.7 fusion.2
  484.0 127.7 %collective-permute-done.6 = bf16[2,512,1536]{2,1,0:T(8,128)(2,1)} collective-permute-done((bf16[2,512,1536]{2,1,0:T(8,128)(2,1)}, bf16[2,512,1536]{2,1,0:T(8,128)(2,1)}, u32[]{:S(2)}, u32[]{:S(2)}) %collective-permute-start.6) | collective-permute-done | bytes 3145760 | tf_op jit(solution)/shard_map/ppermute | solution.py:15
  611.7 2.5 collective-permute-start.7
  614.1 1.0 fusion.91
  615.2 3.0 convolution_add_fusion.4
  618.2 1.1 convolution_add_fusion.3
  619.3 2.9 fusion.86
  622.2 3.0 fusion.14
  625.2 2.9 fusion.83
  628.1 55.4 %collective-permute-done.5 = bf16[2,512,1536]{2,1,0:T(8,128)(2,1)S(1)} collective-permute-done((bf16[2,512,1536]{2,1,0:T(8,128)(2,1)}, bf16[2,512,1536]{2,1,0:T(8,128)(2,1)S(1)}, u32[]{:S(2)}, u32[]{:S(2)}) %collective-permute-start.5) | collective-permute-done | bytes 3145760 | tf_op jit(solution)/shard_map/ppermute | solution.py:17
  683.5 1.0 fusion.13
  684.5 2.6 fusion.15
  687.2 10.6 %convolution_convert_fusion = bf16[256,4096]{1,0:T(8,128)(2,1)} fusion(bf16[1536,4096]{1,0:T(8,128)(2,1)} %all-gather.7.cloned.1.call-done, f32[2,256,1536]{2,1,0:T(8,128)} %fusion.15), kind=kOutput, calls=%fused_computation.8 | convolution fusion | flops 3226206208 | bytes 17825792 | tf_op jit(solution)/shard_map/dot_general | solution.py:127
  697.8 27.6 %reduce-scatter.2.cloned.1.call-done = bf16[256,1024]{1,0:T(8,128)(2,1)} async-done(((bf16[256,4096]{1,0:T(8,128)(2,1)}), bf16[256,1024]{1,0:T(8,128)(2,1)}) %reduce-scatter.2.cloned.1.call-update) | async-done | bytes 524304 | tf_op jit(solution)/shard_map/reduce_scatter | solution.py:132
  725.4 2.0 add_convert_fusion
  (161 shorter events, 2.3 us)
Async XLA Ops:
  7.4 39.1 %copy-start = (bf16[2,2,256,256]{3,2,1,0:T(8,128)(2,1)S(1)}, bf16[2,2,256,256]{3,2,1,0:T(8,128)(2,1)}, u32[]{:S(2)}) copy-start(bf16[2,2,256,256]{3,2,1,0:T(8,128)(2,1)} %param.19) | copy-start | bytes 1572868
  7.4 27.7 %all-gather.5.cloned.1.call-start = ((), (), s32[]{:S(2)}) async-start(), calls=%async_computation.1 | async-start | bytes 2621440 | tf_op jit(solution)/shard_map/all_gather | solution.py:70
  8.1 469.6 %all-reduce.34.cloned.1.call-start = ((), (), s32[]{:S(2)}) async-start(), calls=%async_computation.2 | async-start | bytes 4194304 | tf_op jit(solution)/shard_map/psum | solution.py:108
  37.1 7.6 %copy-start.10 = (f32[512]{0:T(512)S(1)}, f32[512]{0:T(512)}, u32[]{:S(2)}) copy-start(f32[512]{0:T(512)} %param.21) | copy-start | bytes 6148
  37.1 9.0 %copy-start.8 = (f32[512]{0:T(512)S(1)}, f32[512]{0:T(512)}, u32[]{:S(2)}) copy-start(f32[512]{0:T(512)} %param.18) | copy-start | bytes 6148
  41.3 4.7 collective-permute-start
  46.4 1.8 copy-start.9
  58.0 64.1 %copy-start.2 = (bf16[256,4096]{1,0:T(8,128)(2,1)S(1)}, bf16[256,4096]{1,0:T(8,128)(2,1)}, u32[]{:S(2)}) copy-start(bf16[256,4096]{1,0:T(8,128)(2,1)} %all-gather.5.cloned.1.call-done) | copy-start | bytes 6291460
  58.1 64.1 %copy-start.11 = (f32[4096]{0:T(1024)S(1)}, f32[4096]{0:T(1024)}, u32[]{:S(2)}) copy-start(f32[4096]{0:T(1024)} %param.15) | copy-start | bytes 49156
  60.1 62.0 %copy-start.6 = (f32[256,512]{1,0:T(8,128)S(1)}, f32[256,512]{1,0:T(8,128)}, u32[]{:S(2)}) copy-start(f32[256,512]{1,0:T(8,128)} %pad.129) | copy-start | bytes 1572868
  130.1 557.1 %all-gather.7.cloned.1.call-start = ((), (), s32[]{:S(2)}) async-start(), calls=%async_computation.3 | async-start | bytes 14155776 | tf_op jit(solution)/shard_map/all_gather | solution.py:129
  130.6 594.8 %reduce-scatter.2.cloned.1.call-start = ((), (), s32[]{:S(2)}) async-start(), calls=%async_computation.4 | async-start | bytes 2621440 | tf_op jit(solution)/shard_map/reduce_scatter | solution.py:132
  130.7 148.2 %collective-permute-start.2 = (bf16[2,512,1536]{2,1,0:T(8,128)(2,1)}, bf16[2,512,1536]{2,1,0:T(8,128)(2,1)S(1)}, u32[]{:S(2)}, u32[]{:S(2)}) collective-permute-start(bf16[2,512,1536]{2,1,0:T(8,128)(2,1)} %param.24), channel_id=1, source_target_pairs={{0,4},{4,8},{8,12},{12,16},{16,20},{20,24},{24,28},{28,0},{1,5},{5... | collective-permute-start | bytes 9437192 | tf_op jit(solution)/shard_map/ppermute | solution.py:15
  130.8 152.6 %collective-permute-start.1 = (bf16[2,512,1536]{2,1,0:T(8,128)(2,1)}, bf16[2,512,1536]{2,1,0:T(8,128)(2,1)}, u32[]{:S(2)}, u32[]{:S(2)}) collective-permute-start(bf16[2,512,1536]{2,1,0:T(8,128)(2,1)} %param.24), channel_id=1, source_target_pairs={{0,28},{4,0},{8,4},{12,8},{16,12},{20,16},{24,20},{28,24},{1,29},{... | collective-permute-start | bytes 9437192 | tf_op jit(solution)/shard_map/ppermute | solution.py:17
  278.9 1.7 copy-start.3
  280.6 194.5 %collective-permute-start.4 = (bf16[2,512,1536]{2,1,0:T(8,128)(2,1)S(1)}, bf16[2,512,1536]{2,1,0:T(8,128)(2,1)}, u32[]{:S(2)}, u32[]{:S(2)}) collective-permute-start(bf16[2,512,1536]{2,1,0:T(8,128)(2,1)S(1)} %collective-permute-done.2), channel_id=1, source_target_pairs={{0,4},{4,8},{8,12},{12,16},{16,20},{20,24},{24,28},{28,0},{1,5},{5... | collective-permute-start | bytes 9437192 | tf_op jit(solution)/shard_map/ppermute | solution.py:15
  283.3 197.7 %collective-permute-start.3 = (bf16[2,512,1536]{2,1,0:T(8,128)(2,1)}, bf16[2,512,1536]{2,1,0:T(8,128)(2,1)}, u32[]{:S(2)}, u32[]{:S(2)}) collective-permute-start(bf16[2,512,1536]{2,1,0:T(8,128)(2,1)} %collective-permute-done.1), channel_id=1, source_target_pairs={{0,28},{4,0},{8,4},{12,8},{16,12},{20,16},{24,20},{28,24},{1,29},{... | collective-permute-start | bytes 9437192 | tf_op jit(solution)/shard_map/ppermute | solution.py:17
  475.1 136.5 %collective-permute-start.6 = (bf16[2,512,1536]{2,1,0:T(8,128)(2,1)}, bf16[2,512,1536]{2,1,0:T(8,128)(2,1)}, u32[]{:S(2)}, u32[]{:S(2)}) collective-permute-start(bf16[2,512,1536]{2,1,0:T(8,128)(2,1)} %collective-permute-done.4), channel_id=1, source_target_pairs={{0,4},{4,8},{8,12},{12,16},{16,20},{20,24},{24,28},{28,0},{1,5},{5... | collective-permute-start | bytes 9437192 | tf_op jit(solution)/shard_map/ppermute | solution.py:15
  477.7 5.5 copy-start.7
  481.0 133.2 %copy-start.5 = (bf16[2,512,1536]{2,1,0:T(8,128)(2,1)S(1)}, bf16[2,512,1536]{2,1,0:T(8,128)(2,1)}, u32[]{:S(2)}) copy-start(bf16[2,512,1536]{2,1,0:T(8,128)(2,1)} %param.24) | copy-start | bytes 9437188
  481.0 202.5 %collective-permute-start.5 = (bf16[2,512,1536]{2,1,0:T(8,128)(2,1)}, bf16[2,512,1536]{2,1,0:T(8,128)(2,1)S(1)}, u32[]{:S(2)}, u32[]{:S(2)}) collective-permute-start(bf16[2,512,1536]{2,1,0:T(8,128)(2,1)} %collective-permute-done.3), channel_id=1, source_target_pairs={{0,28},{4,0},{8,4},{12,8},{16,12},{20,16},{24,20},{28,24},{1,29},{... | collective-permute-start | bytes 9437192 | tf_op jit(solution)/shard_map/ppermute | solution.py:17
  611.7 72.8 %collective-permute-start.7 = (bf16[2,512,1536]{2,1,0:T(8,128)(2,1)}, bf16[2,512,1536]{2,1,0:T(8,128)(2,1)S(1)}, u32[]{:S(2)}, u32[]{:S(2)}) collective-permute-start(bf16[2,512,1536]{2,1,0:T(8,128)(2,1)} %collective-permute-done.6), channel_id=1, source_target_pairs={{0,4},{4,8},{8,12},{12,16},{16,20},{20,24},{24,28},{28,0},{1,5},{5... | collective-permute-start | bytes 9437192 | tf_op jit(solution)/shard_map/ppermute | solution.py:15
  615.1 3.1 copy-start.4
  687.2 40.3 %copy-start.1 = (bf16[2,2,256,256]{3,2,1,0:T(8,128)(2,1)S(1)}, bf16[2,2,256,256]{3,2,1,0:T(8,128)(2,1)}, u32[]{:S(2)}) copy-start(bf16[2,2,256,256]{3,2,1,0:T(8,128)(2,1)} %param.19) | copy-start | bytes 1572868
Sparse Core Ops, SparseCore 0:
  9.7 25.2 all-gather.4
  130.2 47.6 all-reduce.33
  697.9 27.4 reduce-scatter.1
Sparse Core Ops, SparseCore 1:
  132.6 393.9 all-gather.6
